TPU v7x, 32 devices: a whole 2x2x4 slice. The times are simulated.
32 devices in a mesh: xy: 8 (over y, x, core), gz: 4 (over z).
Axes of the slice: x: 2, y: 2, z: 4, core: 2. Of those that a mesh axis runs over, the one named last changes fastest.
Arguments:
- field: float32 [64, 2, 3, 64, 256], P('gz', None, None, 'xy'), may hold values from -6 to 6
- source: float32 [64, 2, 3, 64, 256], P('gz', None, None, 'xy'), may hold values from -6 to 6
- classes: int32 [64, 64, 256], P('gz', 'xy'), may hold values from 0 to 15
- boundary: int32 [64, 64, 256], P('gz', 'xy'), may hold values 0 or 1
- conductance: float32 [16], replicated, may hold values from 0.001 to 1
- angles: float32 [3], replicated, may hold values from -3.140625 to 3.140625
- strengths: float32 [3], replicated, may hold values from 0.5 to 2
Outputs:
- relaxed: float32 [64, 2, 3, 64, 256], P('gz', None, None, 'xy')
All inputs are finite; a program needn't handle non-finite values. No bound on the sum of `boundary` on one device may be relied on, other than what follows from the above.
Results may differ from a plain program's by a relative error of at most 0.00029.
Values sent between devices are 32-bit elements; how exact they have to be, the bound alone decides.
A program may use at most 64 MiB of HBM per device.

v0:
```python
import functools

import jax
import jax.numpy as jnp
from jax import lax
from jax.experimental import pallas as pl
from jax.experimental.pallas import tpu as pltpu
from jax.sharding import PartitionSpec as P

SWEEPS = 2
PIECES = 2

coupling = 0.1
penalty = 4.0


def mul(a, b):
    return (a[0] * b[0] - a[1] * b[1], a[0] * b[1] + a[1] * b[0])


def add(a, b):
    return (a[0] + b[0], a[1] + b[1])


def inv(a):
    weight = 1.0 / (a[0] * a[0] + a[1] * a[1])
    return (a[0] * weight, -a[1] * weight)


def one_minus(a):
    return (1.0 - a[0], -a[1])


def get(ref, *at):
    return (ref[at + (0,)], ref[at + (1,)])


def put(ref, value, *at):
    ref[at + (0,)] = value[0]
    ref[at + (1,)] = value[1]


def rotation(angles, shape):
    cos = [jnp.cos(jnp.full(shape, angles[i], jnp.float32)) for i in range(3)]
    sin = [jnp.sin(jnp.full(shape, angles[i], jnp.float32)) for i in range(3)]
    (ca, cb, cc), (sa, sb, sc) = cos, sin
    left = [[ca * cb, -sa, ca * sb], [sa * cb, ca, sa * sb], [-sb, jnp.zeros_like(cb), cb]]
    return [[row[0] * cc + row[1] * sc, row[1] * cc - row[0] * sc, row[2]] for row in left]


def relax(
    ngz,
    nxy,
    field,
    source,
    classes,
    boundary,
    conductance,
    angles,
    strengths,
    out,
    U,
    S,
    C,
    B,
    SG,
    DR,
    PH,
    PHI,
    PSI,
    T,
    OUT,
    QM,
    ends,
    coef,
    near,
    halo_out,
    halo_in,
    lam_in,
    lam_out,
    ch_in,
    ch_out,
    in_sems,
    out_sems,
    halo_send,
    halo_recv,
    lam_send,
    lam_recv,
    ch_send,
    ch_recv,
):
    ix, iz = lax.axis_index("xy"), lax.axis_index("gz")
    depth, _, _, rows, width = U.shape
    kinds = conductance.shape[0]
    plane = (rows, width)
    has = {
        ("xy", 0): ix > 0,
        ("xy", 1): ix < nxy - 1,
        ("gz", 0): iz > 0,
        ("gz", 1): iz < ngz - 1,
    }
    where_is = {
        ("xy", 0): ix - 1,
        ("xy", 1): ix + 1,
        ("gz", 0): iz - 1,
        ("gz", 1): iz + 1,
    }
    loads = [
        pltpu.make_async_copy(src, dst, in_sems.at[i])
        for i, (src, dst) in enumerate(((field, U), (classes, C), (boundary, B), (source, S)))
    ]
    for load in loads:
        load.start()

    barrier = pltpu.get_barrier_semaphore()
    for key, there in has.items():

        @pl.when(there)
        def _():
            pl.semaphore_signal(
                barrier,
                inc=1,
                device_id={key[0]: where_is[key]},
                device_id_type=pl.DeviceIdType.MESH,
            )

    count = sum(there.astype(jnp.int32) for there in has.values())
    pl.semaphore_wait(barrier, count)

    def remote(src, dst, send, recv, key):
        return pltpu.make_async_remote_copy(
            src_ref=src,
            dst_ref=dst,
            send_sem=send,
            recv_sem=recv,
            device_id={key[0]: where_is[key]},
            device_id_type=pl.DeviceIdType.MESH,
        )

    zs = depth // PIECES
    lines = zs * 6

    def halo_copy(sweep, side, piece):
        span = pl.ds(piece * lines, lines)
        return remote(
            halo_out.at[sweep, side, span],
            halo_in.at[sweep, side, span],
            halo_send.at[sweep, side, piece],
            halo_recv.at[sweep, side, piece],
            ("xy", 1 - side),
        )

    def send_halo(sweep, piece):
        for side in range(2):

            @pl.when(has["xy", 1 - side])
            def _():
                halo_copy(sweep, side, piece).start()

    def pack(sweep, z, values):
        for i in range(6):
            halo_out[sweep, 0, pl.ds(z * 6 + i, 1), :] = values[i][rows - 1 :, :]
            halo_out[sweep, 1, pl.ds(z * 6 + i, 1), :] = values[i][:1, :]

    for side in range(2):

        @pl.when(jnp.logical_not(has["xy", side]))
        def _():
            for sweep in range(SWEEPS):
                halo_in[sweep, side] = jnp.zeros(halo_in.shape[2:], jnp.float32)

        @pl.when(jnp.logical_not(has["gz", side]))
        def _():
            lam_in[side] = jnp.zeros(lam_in.shape[1:], jnp.float32)
            for sweep in range(SWEEPS):
                for j in range(3):
                    ch_in[sweep, side, j] = jnp.zeros(ch_in.shape[3:], jnp.float32)

    loads[0].wait()
    for piece in range(PIECES):

        def pack_first(k, carry):
            z = piece * zs + k
            pack(0, z, [U[z, i // 3, i % 3] for i in range(6)])
            return carry

        lax.fori_loop(0, zs, pack_first, 0)
        send_halo(0, piece)

    loads[1].wait()
    loads[2].wait()

    def diagonal(z, carry):
        ids = C[z]
        sigma = jnp.zeros(plane, jnp.float32)
        for kind in range(kinds):
            sigma = jnp.where(ids == kind, conductance[kind], sigma)
        SG[z] = sigma
        DR[z] = 2.0 + 4.0 * coupling + penalty * B[z].astype(jnp.float32)
        return carry

    lax.fori_loop(0, depth, diagonal, 0)

    def diag(z):
        real = jnp.broadcast_to(DR[z][None], (3,) + plane)
        sigma = SG[z]
        return real, jnp.stack([sigma * strengths[j] for j in range(3)])

    none = (jnp.zeros((3,) + plane, jnp.float32),) * 2

    def pivots(k, carry):
        p, q = carry
        z, back = k, depth - 1 - k
        d, f = diag(z), diag(back)
        p = inv((d[0] - p[0], d[1] - p[1]))
        q = inv((f[0] - q[0], f[1] - q[1]))
        put(PH, p, z)
        put(PHI, q, back)
        return p, q

    lax.fori_loop(0, depth, pivots, (none, none))
    ones = (jnp.ones((3,) + plane, jnp.float32), none[0])

    def columns(k, carry):
        down, up = carry
        z, back = k, depth - 1 - k
        down = mul(get(PHI, z), down)
        up = mul(get(PH, back), up)
        put(PHI, down, z)
        put(PSI, up, back)
        return down, up

    lax.fori_loop(0, depth, columns, (ones, ones))
    LEFT, RIGHT = 0, 1
    tip = (lambda: get(PHI, 0), lambda: get(PSI, depth - 1))
    across = lambda: get(PSI, 0)

    def lam_copy(side):
        return remote(
            lam_out.at[side],
            lam_in.at[side],
            lam_send.at[side],
            lam_recv.at[side],
            ("gz", 1 - side),
        )

    def pass_lam(side):
        @pl.when(has["gz", side])
        def _():
            lam_copy(side).wait_recv()

        lam = get(lam_in, side)
        kappa = mul(across(), inv(one_minus(mul(tip[side](), lam))))
        both = mul(kappa, lam)
        put(coef, kappa, side)
        put(coef, both, 2 + side)
        put(lam_out, add(tip[1 - side](), mul(across(), both)), side)

        @pl.when(has["gz", 1 - side])
        def _():
            lam_copy(side).start()

    def chain_copy(sweep, side, j):
        return remote(
            ch_out.at[sweep, side, j],
            ch_in.at[sweep, side, j],
            ch_send.at[sweep, side, j],
            ch_recv.at[sweep, side, j],
            ("gz", 1 - side),
        )

    def pass_chain(sweep, side):
        for j in range(3):
            base = add(
                (ends[1 - side, 0, j], ends[1 - side, 1, j]),
                mul(
                    (coef[2 + side, 0, j], coef[2 + side, 1, j]),
                    (ends[side, 0, j], ends[side, 1, j]),
                ),
            )

            @pl.when(has["gz", side])
            def _():
                chain_copy(sweep, side, j).wait_recv()

            result = add(
                base,
                mul(
                    (coef[side, 0, j], coef[side, 1, j]),
                    (ch_in[sweep, side, j, 0], ch_in[sweep, side, j, 1]),
                ),
            )
            ch_out[sweep, side, j, 0] = result[0]
            ch_out[sweep, side, j, 1] = result[1]

            @pl.when(has["gz", 1 - side])
            def _():
                chain_copy(sweep, side, j).start()

    left_first = iz * 2 < ngz - 1

    def near_side(run):
        @pl.when(left_first)
        def _():
            run(LEFT)

        @pl.when(jnp.logical_not(left_first))
        def _():
            run(RIGHT)

    def far_side(run):
        @pl.when(left_first)
        def _():
            run(RIGHT)

        @pl.when(jnp.logical_not(left_first))
        def _():
            run(LEFT)

    @pl.when(jnp.logical_not(has["gz", 0]))
    def _():
        pass_lam(LEFT)

    @pl.when(jnp.logical_not(has["gz", 1]))
    def _():
        pass_lam(RIGHT)

    angle_matrix = rotation(angles, (rows, 128))
    for c in range(3):
        for j in range(3):
            QM[c, j] = angle_matrix[c][j]

    def matrix():
        return [
            [jnp.concatenate([QM[c, j]] * (width // 128), axis=1) for j in range(3)]
            for c in range(3)
        ]

    row = lax.broadcasted_iota(jnp.int32, plane, 0)
    lane = lax.broadcasted_iota(jnp.int32, plane, 1)
    zero = jnp.zeros(plane, jnp.float32)

    def turn(q, driven):
        return [
            jnp.stack(
                [
                    q[0][j] * driven[p][0] + q[1][j] * driven[p][1] + q[2][j] * driven[p][2]
                    for j in range(3)
                ]
            )
            for p in range(2)
        ]

    def inner(z, carry):
        first, last = carry
        q = matrix()
        driven = []
        for p in range(2):
            of = []
            for c in range(3):
                u = U[z, p, c]
                beside = jnp.where(lane == 0, zero, pltpu.roll(u, 1, 1))
                beside += jnp.where(lane == width - 1, zero, pltpu.roll(u, width - 1, 1))
                beside += jnp.where(row == 0, zero, pltpu.roll(u, 1, 0))
                beside += jnp.where(row == rows - 1, zero, pltpu.roll(u, rows - 1, 0))
                of.append(S[z, p, c] + coupling * beside)
            driven.append(of)
        turned = turn(q, driven)
        put(T, turned, z)
        return add(first, mul(get(PHI, z), turned)), add(last, mul(get(PSI, z), turned))

    def outer(sweep, z, carry):
        first, last = carry
        q = matrix()
        driven = []
        for p in range(2):
            of = []
            for c in range(3):
                at = pl.ds(z * 6 + p * 3 + c, 1)
                above = jnp.broadcast_to(halo_in[sweep, 0, at, :], plane)
                below = jnp.broadcast_to(halo_in[sweep, 1, at, :], plane)
                edge = jnp.where(row == 0, above, zero) + jnp.where(row == rows - 1, below, zero)
                of.append(coupling * edge)
            driven.append(of)
        turned = turn(q, driven)
        put(T, add(get(T, z), turned), z)
        return add(first, mul(get(PHI, z), turned)), add(last, mul(get(PSI, z), turned))

    loads[3].wait()
    for sweep in range(SWEEPS):
        sums = lax.fori_loop(0, depth, inner, (none, none))
        for piece in range(PIECES):
            for side in range(2):

                @pl.when(has["xy", side])
                def _():
                    halo_copy(sweep, side, piece).wait_recv()

            sums = lax.fori_loop(
                piece * zs, (piece + 1) * zs, functools.partial(outer, sweep), sums
            )
        put(ends, sums[0], 0)
        put(ends, sums[1], 1)

        if sweep == 0:
            def late(side):
                @pl.when(has["gz", side])
                def _():
                    pass_lam(side)

            near_side(late)
            near_side(lambda side: pass_chain(0, side))
        else:
            near_side(lambda side: pass_chain(1, side))

        def forward(z, m):
            m = mul(get(PH, z), add(get(T, z), m))
            put(T, m, z)
            return m

        def backward(k, w):
            z = depth - 1 - k
            w = add(get(T, z), mul(get(PH, z), w))
            put(T, w, z)
            return w

        if sweep == 0:
            far_side(late)
        lax.fori_loop(0, depth, forward, none)
        lax.fori_loop(0, depth, backward, none)
        if sweep == 0:
            for side in range(2):
                lam, away = get(lam_in, side), get(lam_out, 1 - side)
                det = inv(one_minus(mul(lam, away)))
                put(coef, det, 6 + side)
                put(coef, mul(det, lam), 4 + side)
        far_side(functools.partial(pass_chain, sweep))

        for side in range(2):
            for j in range(3):
                arrived = (ch_in[sweep, side, j, 0], ch_in[sweep, side, j, 1])
                other = (ch_out[sweep, 1 - side, j, 0], ch_out[sweep, 1 - side, j, 1])
                value = add(
                    mul((coef[6 + side, 0, j], coef[6 + side, 1, j]), arrived),
                    mul((coef[4 + side, 0, j], coef[4 + side, 1, j]), other),
                )
                near[side, 0, j] = value[0]
                near[side, 1, j] = value[1]

        final = sweep == SWEEPS - 1

        def join(z, carry):
            q = matrix()
            before, after = get(near, 0), get(near, 1)
            w = add(add(get(T, z), mul(get(PHI, z), before)), mul(get(PSI, z), after))
            values = []
            for p in range(2):
                for c in range(3):
                    values.append(q[c][0] * w[p][0] + q[c][1] * w[p][1] + q[c][2] * w[p][2])
            target = OUT if final else U
            for i in range(6):
                target[z, i // 3, i % 3] = values[i]
            if not final:
                pack(sweep + 1, z, values)
            return carry

        for piece in range(PIECES):
            lax.fori_loop(piece * zs, (piece + 1) * zs, join, 0)
            if final:
                span = pl.ds(piece * zs, zs)
                pltpu.make_async_copy(OUT.at[span], out.at[span], out_sems.at[piece]).start()
            else:
                send_halo(sweep + 1, piece)

    for side in range(2):

        @pl.when(has["xy", 1 - side])
        def _():
            for sweep in range(SWEEPS):
                for piece in range(PIECES):
                    halo_copy(sweep, side, piece).wait_send()

        @pl.when(has["gz", 1 - side])
        def _():
            lam_copy(side).wait_send()
            for sweep in range(SWEEPS):
                for j in range(3):
                    chain_copy(sweep, side, j).wait_send()

    for piece in range(PIECES):
        span = pl.ds(piece * zs, zs)
        pltpu.make_async_copy(OUT.at[span], out.at[span], out_sems.at[piece]).wait()


def local(ngz, nxy, field, source, classes, boundary, conductance, angles, strengths):
    depth, _, _, rows, width = field.shape
    f32 = jnp.float32
    block = pltpu.VMEM(field.shape, f32)
    flat = (depth, rows, width)
    line = (2, 3, rows, width)
    dma = pltpu.SemaphoreType.DMA
    hbm = pl.BlockSpec(memory_space=pl.ANY)
    smem = pl.BlockSpec(memory_space=pltpu.SMEM)
    return pl.pallas_call(
        functools.partial(relax, ngz, nxy),
        out_shape=jax.ShapeDtypeStruct(field.shape, f32),
        in_specs=[hbm] * 4 + [smem] * 3,
        out_specs=hbm,
        scratch_shapes=[
            block,
            block,
            pltpu.VMEM(flat, jnp.int32),
            pltpu.VMEM(flat, jnp.int32),
            pltpu.VMEM(flat, f32),
            pltpu.VMEM(flat, f32),
            block,
            block,
            block,
            block,
            block,
            pltpu.VMEM((3, 3, rows, 128), f32),
            pltpu.VMEM((2,) + line, f32),
            pltpu.VMEM((8,) + line, f32),
            pltpu.VMEM((2,) + line, f32),
            pltpu.VMEM((SWEEPS, 2, depth * 6, width), f32),
            pltpu.VMEM((SWEEPS, 2, depth * 6, width), f32),
            pltpu.VMEM((2,) + line, f32),
            pltpu.VMEM((2,) + line, f32),
            pltpu.VMEM((SWEEPS, 2, 3, 2, rows, width), f32),
            pltpu.VMEM((SWEEPS, 2, 3, 2, rows, width), f32),
            dma((4,)),
            dma((PIECES,)),
            dma((SWEEPS, 2, PIECES)),
            dma((SWEEPS, 2, PIECES)),
            dma((2,)),
            dma((2,)),
            dma((SWEEPS, 2, 3)),
            dma((SWEEPS, 2, 3)),
        ],
        compiler_params=pltpu.CompilerParams(collective_id=0, has_side_effects=True),
    )(field, source, classes, boundary, conductance, angles, strengths)


def solution(mesh):
    in_specs = (
        P("gz", None, None, "xy", None),
        P("gz", None, None, "xy", None),
        P("gz", "xy", None),
        P("gz", "xy", None),
        P(),
        P(),
        P(),
    )
    out_specs = P("gz", None, None, "xy", None)
    body = functools.partial(local, mesh.shape["gz"], mesh.shape["xy"])
    return jax.shard_map(body, mesh=mesh, in_specs=in_specs, out_specs=out_specs, check_vma=False)
```

profile of v0, /device:TPU:0, one launch (start us, length us, event | category | flops | bytes accessed | tf_op | source)
XLA Modules:
  0.0 32.5 jit_solution(11276853208509664112)
XLA Ops:
  0.0 30.4 %shard_map.73 = f32[16,2,3,8,256]{4,3,2,1,0:T(8,128)} custom-call(f32[16,2,3,8,256]{4,3,2,1,0:T(8,128)} %field.1, f32[16,2,3,8,256]{4,3,2,1,0:T(8,128)} %source.1, s32[16,8,256]{2,1,0:T(8,128)} %classes.1, s32[16,8,256]{2,1,0:T(8,128)} %boundary.1, f32[16]{0:T(128)} %conductance.1, f32[3]{0:T(128)} %angles.1, f32[3]{0:T(128)} %strengths.1), custom_call_target="tpu_custom_call" | custom-call | tf_op jit(solution)/shard_map/pallas_call | solution.py:504
  30.4 2.1 %copy.9 = f32[16,2,3,8,256]{4,3,2,1,0:T(8,128)} copy(f32[16,2,3,8,256]{4,3,2,1,0:T(8,128)} %shard_map.73) | data formatting | bytes 1572864
where the time goes:
time: 32.6 us; the launch traced here: 32.5 us
  Pallas kernels  30.4 us (93%)
  local copies, waits for them, and re-layouts  2.06 us (6%)
    pallas_call x1, Pallas kernels, local(): pl.pallas_call(functools.partial(relax, ngz, nxy), out_shape=jax.ShapeDty...  30.4 us
    unnamed x1, local copies, waits for them, and re-layouts  2.06 us

commit v1 on v0

--- a/solution.py
+++ b/solution.py
@@ -76,16 +76,25 @@
     near,
     halo_out,
     halo_in,
+    value_in,
+    info_in,
+    info_out,
     lam_in,
     lam_out,
+    own_in,
+    own_out,
     ch_in,
     ch_out,
     in_sems,
     out_sems,
     halo_send,
     halo_recv,
+    info_send,
+    info_recv,
     lam_send,
     lam_recv,
+    own_send,
+    own_recv,
     ch_send,
     ch_recv,
 ):
@@ -96,15 +105,17 @@
     has = {
         ("xy", 0): ix > 0,
         ("xy", 1): ix < nxy - 1,
-        ("gz", 0): iz > 0,
-        ("gz", 1): iz < ngz - 1,
     }
     where_is = {
         ("xy", 0): ix - 1,
         ("xy", 1): ix + 1,
-        ("gz", 0): iz - 1,
-        ("gz", 1): iz + 1,
     }
+    for steps in (1, 2):
+        has["gz", -steps] = iz >= steps
+        has["gz", steps] = iz < ngz - steps
+        where_is["gz", -steps] = iz - steps
+        where_is["gz", steps] = iz + steps
+
     loads = [
         pltpu.make_async_copy(src, dst, in_sems.at[i])
         for i, (src, dst) in enumerate(((field, U), (classes, C), (boundary, B), (source, S)))
@@ -162,6 +173,7 @@
             halo_out[sweep, 0, pl.ds(z * 6 + i, 1), :] = values[i][rows - 1 :, :]
             halo_out[sweep, 1, pl.ds(z * 6 + i, 1), :] = values[i][:1, :]
 
+
     for side in range(2):
 
         @pl.when(jnp.logical_not(has["xy", side]))
@@ -169,13 +181,16 @@
             for sweep in range(SWEEPS):
                 halo_in[sweep, side] = jnp.zeros(halo_in.shape[2:], jnp.float32)
 
-        @pl.when(jnp.logical_not(has["gz", side]))
-        def _():
+        @pl.when((iz if side == 0 else ngz - 1 - iz) < 2)
+        def _():
+            for part in range(3, 9):
+                info_in[side, part] = jnp.zeros(info_in.shape[2:], jnp.float32)
             lam_in[side] = jnp.zeros(lam_in.shape[1:], jnp.float32)
             for sweep in range(SWEEPS):
                 for j in range(3):
                     ch_in[sweep, side, j] = jnp.zeros(ch_in.shape[3:], jnp.float32)
 
+
     loads[0].wait()
     for piece in range(PIECES):
 
@@ -186,6 +201,7 @@
 
         lax.fori_loop(0, zs, pack_first, 0)
         send_halo(0, piece)
+
 
     loads[1].wait()
     loads[2].wait()
@@ -218,6 +234,7 @@
         put(PHI, q, back)
         return p, q
 
+
     lax.fori_loop(0, depth, pivots, (none, none))
     ones = (jnp.ones((3,) + plane, jnp.float32), none[0])
 
@@ -230,46 +247,135 @@
         put(PSI, up, back)
         return down, up
 
+
     lax.fori_loop(0, depth, columns, (ones, ones))
     LEFT, RIGHT = 0, 1
     tip = (lambda: get(PHI, 0), lambda: get(PSI, depth - 1))
     across = lambda: get(PSI, 0)
 
-    def lam_copy(side):
-        return remote(
-            lam_out.at[side],
-            lam_in.at[side],
-            lam_send.at[side],
-            lam_recv.at[side],
-            ("gz", 1 - side),
+    place = (iz, ngz - 1 - iz)
+    even = [lax.rem(k, 2) == 0 for k in place]
+    odd = [lax.rem(k, 2) == 1 for k in place]
+    onward = [ngz - 1 - k for k in place]
+
+    def to(side, steps):
+        return {"gz": iz + steps if side == LEFT else iz - steps}
+
+    def chain_copy(src, dst, send, recv, side, steps):
+        return pltpu.make_async_remote_copy(
+            src_ref=src,
+            dst_ref=dst,
+            send_sem=send,
+            recv_sem=recv,
+            device_id=to(side, steps),
+            device_id_type=pl.DeviceIdType.MESH,
         )
 
-    def pass_lam(side):
-        @pl.when(has["gz", side])
-        def _():
-            lam_copy(side).wait_recv()
-
-        lam = get(lam_in, side)
-        kappa = mul(across(), inv(one_minus(mul(tip[side](), lam))))
-        both = mul(kappa, lam)
-        put(coef, kappa, side)
-        put(coef, both, 2 + side)
-        put(lam_out, add(tip[1 - side](), mul(across(), both)), side)
-
-        @pl.when(has["gz", 1 - side])
-        def _():
-            lam_copy(side).start()
-
-    def chain_copy(sweep, side, j):
-        return remote(
+    def info_copy(side, j):
+        return chain_copy(
+            info_out.at[side, j],
+            info_in.at[side, j],
+            info_send.at[side, j],
+            info_recv.at[side, j],
+            side,
+            1,
+        )
+
+    def lam_copy(side, steps, j):
+        return chain_copy(
+            lam_out.at[side, j],
+            lam_in.at[side, j],
+            lam_send.at[side, steps - 1, j],
+            lam_recv.at[side, j],
+            side,
+            steps,
+        )
+
+    def own_copy(sweep, side, j):
+        return chain_copy(
+            own_out.at[sweep, side, j],
+            own_in.at[sweep, side, j],
+            own_send.at[sweep, side, j],
+            own_recv.at[sweep, side, j],
+            side,
+            1,
+        )
+
+    def x_copy(sweep, side, steps, j):
+        return chain_copy(
             ch_out.at[sweep, side, j],
             ch_in.at[sweep, side, j],
-            ch_send.at[sweep, side, j],
+            ch_send.at[sweep, side, steps - 1, j],
             ch_recv.at[sweep, side, j],
-            ("gz", 1 - side),
+            side,
+            steps,
         )
 
-    def pass_chain(sweep, side):
+    both = jnp.logical_and
+
+    def send_info(side):
+        parts = (tip[1 - side](), tip[side](), across())
+        for part in range(3):
+            for j in range(3):
+                for p in range(2):
+                    info_out[side, part * 3 + j, p] = parts[part][p][j]
+            sends = both(even[side], onward[side] >= 1)
+
+            @pl.when(sends if part == 0 else both(sends, place[side] > 0))
+            def _():
+                for j in range(3):
+                    info_copy(side, part * 3 + j).start()
+
+    def pass_lam(side):
+        @pl.when(odd[side])
+        def _():
+            for j in range(3):
+                info_copy(side, j).wait_recv()
+
+        @pl.when(both(odd[side], place[side] >= 2))
+        def _():
+            for j in range(3, 9):
+                info_copy(side, j).wait_recv()
+
+        @pl.when(place[side] >= 2)
+        def _():
+            for j in range(3):
+                lam_copy(side, 1, j).wait_recv()
+
+        for j in range(3):
+            tips = [(info_in[side, 3 * k + j, 0], info_in[side, 3 * k + j, 1]) for k in range(3)]
+            given = (lam_in[side, j, 0], lam_in[side, j, 1])
+
+            @pl.when(odd[side])
+            def _():
+                skip = mul(tips[2], inv(one_minus(mul(tips[1], given))))
+                lam = add(tips[0], mul(tips[2], mul(skip, given)))
+                for p in range(2):
+                    coef[8 + side, p, j] = skip[p]
+                    coef[10 + side, p, j] = lam[p]
+
+            @pl.when(even[side])
+            def _():
+                for p in range(2):
+                    coef[10 + side, p, j] = given[p]
+
+            of = lambda pair: (pair[0][j], pair[1][j])
+            lam = (coef[10 + side, 0, j], coef[10 + side, 1, j])
+            kappa = mul(of(across()), inv(one_minus(mul(of(tip[side]()), lam))))
+            over = mul(kappa, lam)
+            value = add(of(tip[1 - side]()), mul(of(across()), over))
+            for p in range(2):
+                coef[side, p, j] = kappa[p]
+                coef[2 + side, p, j] = over[p]
+                lam_out[side, j, p] = value[p]
+
+            for steps in (2, 1):
+
+                @pl.when(both(odd[side], onward[side] >= steps))
+                def _():
+                    lam_copy(side, steps, j).start()
+
+    def own_sum(sweep, side):
         for j in range(3):
             base = add(
                 (ends[1 - side, 0, j], ends[1 - side, 1, j]),
@@ -278,24 +384,49 @@
                     (ends[side, 0, j], ends[side, 1, j]),
                 ),
             )
-
-            @pl.when(has["gz", side])
-            def _():
-                chain_copy(sweep, side, j).wait_recv()
-
-            result = add(
-                base,
-                mul(
-                    (coef[side, 0, j], coef[side, 1, j]),
-                    (ch_in[sweep, side, j, 0], ch_in[sweep, side, j, 1]),
-                ),
-            )
-            ch_out[sweep, side, j, 0] = result[0]
-            ch_out[sweep, side, j, 1] = result[1]
-
-            @pl.when(has["gz", 1 - side])
-            def _():
-                chain_copy(sweep, side, j).start()
+            for p in range(2):
+                own_out[sweep, side, j, p] = base[p]
+
+            @pl.when(both(even[side], onward[side] >= 1))
+            def _():
+                own_copy(sweep, side, j).start()
+
+    def pass_chain(sweep, side):
+        for j in range(3):
+
+            @pl.when(odd[side])
+            def _():
+                own_copy(sweep, side, j).wait_recv()
+
+            @pl.when(place[side] >= 2)
+            def _():
+                x_copy(sweep, side, 1, j).wait_recv()
+
+            given = (ch_in[sweep, side, j, 0], ch_in[sweep, side, j, 1])
+
+            @pl.when(odd[side])
+            def _():
+                own = (own_in[sweep, side, j, 0], own_in[sweep, side, j, 1])
+                x = add(own, mul((coef[8 + side, 0, j], coef[8 + side, 1, j]), given))
+                for p in range(2):
+                    value_in[side, j, p] = x[p]
+
+            @pl.when(even[side])
+            def _():
+                for p in range(2):
+                    value_in[side, j, p] = given[p]
+
+            x = (value_in[side, j, 0], value_in[side, j, 1])
+            base = (own_out[sweep, side, j, 0], own_out[sweep, side, j, 1])
+            result = add(base, mul((coef[side, 0, j], coef[side, 1, j]), x))
+            for p in range(2):
+                ch_out[sweep, side, j, p] = result[p]
+
+            for steps in (2, 1):
+
+                @pl.when(both(odd[side], onward[side] >= steps))
+                def _():
+                    x_copy(sweep, side, steps, j).start()
 
     left_first = iz * 2 < ngz - 1
 
@@ -317,13 +448,10 @@
         def _():
             run(LEFT)
 
-    @pl.when(jnp.logical_not(has["gz", 0]))
-    def _():
-        pass_lam(LEFT)
-
-    @pl.when(jnp.logical_not(has["gz", 1]))
-    def _():
-        pass_lam(RIGHT)
+
+    near_side(send_info)
+    far_side(send_info)
+
 
     angle_matrix = rotation(angles, (rows, 128))
     for c in range(3):
@@ -386,9 +514,12 @@
         put(T, add(get(T, z), turned), z)
         return add(first, mul(get(PHI, z), turned)), add(last, mul(get(PSI, z), turned))
 
+
     loads[3].wait()
     for sweep in range(SWEEPS):
+
         sums = lax.fori_loop(0, depth, inner, (none, none))
+
         for piece in range(PIECES):
             for side in range(2):
 
@@ -402,16 +533,16 @@
         put(ends, sums[0], 0)
         put(ends, sums[1], 1)
 
+
         if sweep == 0:
-            def late(side):
-                @pl.when(has["gz", side])
-                def _():
-                    pass_lam(side)
-
-            near_side(late)
-            near_side(lambda side: pass_chain(0, side))
-        else:
-            near_side(lambda side: pass_chain(1, side))
+            near_side(pass_lam)
+        near_side(functools.partial(own_sum, sweep))
+        if sweep > 0:
+            far_side(functools.partial(own_sum, sweep))
+        near_side(functools.partial(pass_chain, sweep))
+        if sweep == 0:
+            far_side(pass_lam)
+            far_side(functools.partial(own_sum, sweep))
 
         def forward(z, m):
             m = mul(get(PH, z), add(get(T, z), m))
@@ -424,21 +555,25 @@
             put(T, w, z)
             return w
 
-        if sweep == 0:
-            far_side(late)
+
         lax.fori_loop(0, depth, forward, none)
         lax.fori_loop(0, depth, backward, none)
+
         if sweep == 0:
             for side in range(2):
-                lam, away = get(lam_in, side), get(lam_out, 1 - side)
+                lam = get(coef, 10 + side)
+                away = tuple(
+                    jnp.stack([lam_out[1 - side, j, p] for j in range(3)]) for p in range(2)
+                )
                 det = inv(one_minus(mul(lam, away)))
                 put(coef, det, 6 + side)
                 put(coef, mul(det, lam), 4 + side)
         far_side(functools.partial(pass_chain, sweep))
 
+
         for side in range(2):
             for j in range(3):
-                arrived = (ch_in[sweep, side, j, 0], ch_in[sweep, side, j, 1])
+                arrived = (value_in[side, j, 0], value_in[side, j, 1])
                 other = (ch_out[sweep, 1 - side, j, 0], ch_out[sweep, 1 - side, j, 1])
                 value = add(
                     mul((coef[6 + side, 0, j], coef[6 + side, 1, j]), arrived),
@@ -464,6 +599,7 @@
                 pack(sweep + 1, z, values)
             return carry
 
+
         for piece in range(PIECES):
             lax.fori_loop(piece * zs, (piece + 1) * zs, join, 0)
             if final:
@@ -472,6 +608,7 @@
             else:
                 send_halo(sweep + 1, piece)
 
+
     for side in range(2):
 
         @pl.when(has["xy", 1 - side])
@@ -480,12 +617,28 @@
                 for piece in range(PIECES):
                     halo_copy(sweep, side, piece).wait_send()
 
-        @pl.when(has["gz", 1 - side])
-        def _():
-            lam_copy(side).wait_send()
-            for sweep in range(SWEEPS):
+        sends = both(even[side], onward[side] >= 1)
+
+        @pl.when(sends)
+        def _():
+            for j in range(3):
+                info_copy(side, j).wait_send()
+                for sweep in range(SWEEPS):
+                    own_copy(sweep, side, j).wait_send()
+
+        @pl.when(both(sends, place[side] > 0))
+        def _():
+            for j in range(3, 9):
+                info_copy(side, j).wait_send()
+
+        for steps in (2, 1):
+
+            @pl.when(both(odd[side], onward[side] >= steps))
+            def _():
                 for j in range(3):
-                    chain_copy(sweep, side, j).wait_send()
+                    lam_copy(side, steps, j).wait_send()
+                    for sweep in range(SWEEPS):
+                        x_copy(sweep, side, steps, j).wait_send()
 
     for piece in range(PIECES):
         span = pl.ds(piece * zs, zs)
@@ -498,6 +651,7 @@
     block = pltpu.VMEM(field.shape, f32)
     flat = (depth, rows, width)
     line = (2, 3, rows, width)
+    pair = (2, rows, width)
     dma = pltpu.SemaphoreType.DMA
     hbm = pl.BlockSpec(memory_space=pl.ANY)
     smem = pl.BlockSpec(memory_space=pltpu.SMEM)
@@ -520,21 +674,30 @@
             block,
             pltpu.VMEM((3, 3, rows, 128), f32),
             pltpu.VMEM((2,) + line, f32),
-            pltpu.VMEM((8,) + line, f32),
+            pltpu.VMEM((12,) + line, f32),
             pltpu.VMEM((2,) + line, f32),
             pltpu.VMEM((SWEEPS, 2, depth * 6, width), f32),
             pltpu.VMEM((SWEEPS, 2, depth * 6, width), f32),
-            pltpu.VMEM((2,) + line, f32),
-            pltpu.VMEM((2,) + line, f32),
-            pltpu.VMEM((SWEEPS, 2, 3, 2, rows, width), f32),
-            pltpu.VMEM((SWEEPS, 2, 3, 2, rows, width), f32),
+            pltpu.VMEM((2, 3) + pair, f32),
+            pltpu.VMEM((2, 9) + pair, f32),
+            pltpu.VMEM((2, 9) + pair, f32),
+            pltpu.VMEM((2, 3) + pair, f32),
+            pltpu.VMEM((2, 3) + pair, f32),
+            pltpu.VMEM((SWEEPS, 2, 3) + pair, f32),
+            pltpu.VMEM((SWEEPS, 2, 3) + pair, f32),
+            pltpu.VMEM((SWEEPS, 2, 3) + pair, f32),
+            pltpu.VMEM((SWEEPS, 2, 3) + pair, f32),
             dma((4,)),
             dma((PIECES,)),
             dma((SWEEPS, 2, PIECES)),
             dma((SWEEPS, 2, PIECES)),
-            dma((2,)),
-            dma((2,)),
+            dma((2, 9)),
+            dma((2, 9)),
+            dma((2, 2, 3)),
+            dma((2, 3)),
             dma((SWEEPS, 2, 3)),
+            dma((SWEEPS, 2, 3)),
+            dma((SWEEPS, 2, 2, 3)),
             dma((SWEEPS, 2, 3)),
         ],
         compiler_params=pltpu.CompilerParams(collective_id=0, has_side_effects=True),

time: 32.6 us -> 32.7 us (level)
  no operation moved by 1% of the time
where the time goes in v1:
time: 32.7 us; the launch traced here: 32.5 us
  Pallas kernels  30.5 us (93%)
  local copies, waits for them, and re-layouts  2.06 us (6%)
    pallas_call x1, Pallas kernels, local(): pl.pallas_call(functools.partial(relax, ngz, nxy), out_shape=jax.ShapeDty...  30.5 us
    unnamed x1, local copies, waits for them, and re-layouts  2.06 us

profile of v1, /device:TPU:0, one launch (start us, length us, event | category | flops | bytes accessed | tf_op | source)
XLA Modules:
  0.0 32.5 jit_solution(10978206011918259001)
XLA Ops:
  0.0 30.5 %shard_map.73 = f32[16,2,3,8,256]{4,3,2,1,0:T(8,128)} custom-call(f32[16,2,3,8,256]{4,3,2,1,0:T(8,128)} %field.1, f32[16,2,3,8,256]{4,3,2,1,0:T(8,128)} %source.1, s32[16,8,256]{2,1,0:T(8,128)} %classes.1, s32[16,8,256]{2,1,0:T(8,128)} %boundary.1, f32[16]{0:T(128)} %conductance.1, f32[3]{0:T(128)} %angles.1, f32[3]{0:T(128)} %strengths.1), custom_call_target="tpu_custom_call" | custom-call | tf_op jit(solution)/shard_map/pallas_call | solution.py:658
  30.5 2.1 %copy.9 = f32[16,2,3,8,256]{4,3,2,1,0:T(8,128)} copy(f32[16,2,3,8,256]{4,3,2,1,0:T(8,128)} %shard_map.73) | data formatting | bytes 1572864

commit v2 on v1

--- a/solution.py
+++ b/solution.py
@@ -38,6 +38,17 @@
 def put(ref, value, *at):
     ref[at + (0,)] = value[0]
     ref[at + (1,)] = value[1]
+
+
+def loop(low, high, body, carry, by):
+    by = by if (high - low) % by == 0 else 1
+
+    def several(k, carry):
+        for i in range(by):
+            carry = body(low + k * by + i, carry)
+        return carry
+
+    return lax.fori_loop(0, (high - low) // by, several, carry)
 
 
 def rotation(angles, shape):
@@ -81,6 +92,8 @@
     info_out,
     lam_in,
     lam_out,
+    extra_in,
+    extra_out,
     own_in,
     own_out,
     ch_in,
@@ -93,6 +106,8 @@
     info_recv,
     lam_send,
     lam_recv,
+    extra_send,
+    extra_recv,
     own_send,
     own_recv,
     ch_send,
@@ -115,7 +130,6 @@
         has["gz", steps] = iz < ngz - steps
         where_is["gz", -steps] = iz - steps
         where_is["gz", steps] = iz + steps
-
     loads = [
         pltpu.make_async_copy(src, dst, in_sems.at[i])
         for i, (src, dst) in enumerate(((field, U), (classes, C), (boundary, B), (source, S)))
@@ -135,8 +149,6 @@
                 device_id_type=pl.DeviceIdType.MESH,
             )
 
-    count = sum(there.astype(jnp.int32) for there in has.values())
-    pl.semaphore_wait(barrier, count)
 
     def remote(src, dst, send, recv, key):
         return pltpu.make_async_remote_copy(
@@ -173,7 +185,6 @@
             halo_out[sweep, 0, pl.ds(z * 6 + i, 1), :] = values[i][rows - 1 :, :]
             halo_out[sweep, 1, pl.ds(z * 6 + i, 1), :] = values[i][:1, :]
 
-
     for side in range(2):
 
         @pl.when(jnp.logical_not(has["xy", side]))
@@ -185,23 +196,23 @@
         def _():
             for part in range(3, 9):
                 info_in[side, part] = jnp.zeros(info_in.shape[2:], jnp.float32)
+            extra_in[side] = jnp.zeros(extra_in.shape[1:], jnp.float32)
             lam_in[side] = jnp.zeros(lam_in.shape[1:], jnp.float32)
             for sweep in range(SWEEPS):
                 for j in range(3):
                     ch_in[sweep, side, j] = jnp.zeros(ch_in.shape[3:], jnp.float32)
 
-
     loads[0].wait()
+
+    def pack_first(z, carry):
+        pack(0, z, [U[z, i // 3, i % 3] for i in range(6)])
+        return carry
+
+    loop(0, depth, pack_first, 0, 4)
+    count = sum(there.astype(jnp.int32) for there in has.values())
+    pl.semaphore_wait(barrier, count)
     for piece in range(PIECES):
-
-        def pack_first(k, carry):
-            z = piece * zs + k
-            pack(0, z, [U[z, i // 3, i % 3] for i in range(6)])
-            return carry
-
-        lax.fori_loop(0, zs, pack_first, 0)
         send_halo(0, piece)
-
 
     loads[1].wait()
     loads[2].wait()
@@ -215,7 +226,7 @@
         DR[z] = 2.0 + 4.0 * coupling + penalty * B[z].astype(jnp.float32)
         return carry
 
-    lax.fori_loop(0, depth, diagonal, 0)
+    loop(0, depth, diagonal, 0, 4)
 
     def diag(z):
         real = jnp.broadcast_to(DR[z][None], (3,) + plane)
@@ -234,8 +245,7 @@
         put(PHI, q, back)
         return p, q
 
-
-    lax.fori_loop(0, depth, pivots, (none, none))
+    loop(0, depth, pivots, (none, none), 2)
     ones = (jnp.ones((3,) + plane, jnp.float32), none[0])
 
     def columns(k, carry):
@@ -247,8 +257,7 @@
         put(PSI, up, back)
         return down, up
 
-
-    lax.fori_loop(0, depth, columns, (ones, ones))
+    loop(0, depth, columns, (ones, ones), 2)
     LEFT, RIGHT = 0, 1
     tip = (lambda: get(PHI, 0), lambda: get(PSI, depth - 1))
     across = lambda: get(PSI, 0)
@@ -349,8 +358,10 @@
             @pl.when(odd[side])
             def _():
                 skip = mul(tips[2], inv(one_minus(mul(tips[1], given))))
-                lam = add(tips[0], mul(tips[2], mul(skip, given)))
+                along = mul(skip, given)
+                lam = add(tips[0], mul(tips[2], along))
                 for p in range(2):
+                    coef[12 + side, p, j] = along[p]
                     coef[8 + side, p, j] = skip[p]
                     coef[10 + side, p, j] = lam[p]
 
@@ -375,29 +386,61 @@
                 def _():
                     lam_copy(side, steps, j).start()
 
+    def extra_copy(side, j):
+        return chain_copy(
+            extra_out.at[side, j],
+            extra_in.at[side, j],
+            extra_send.at[side, j],
+            extra_recv.at[side, j],
+            side,
+            1,
+        )
+
+    def own_base(side, j):
+        return add(
+            (ends[1 - side, 0, j], ends[1 - side, 1, j]),
+            mul(
+                (coef[2 + side, 0, j], coef[2 + side, 1, j]),
+                (ends[side, 0, j], ends[side, 1, j]),
+            ),
+        )
+
     def own_sum(sweep, side):
         for j in range(3):
-            base = add(
-                (ends[1 - side, 0, j], ends[1 - side, 1, j]),
-                mul(
-                    (coef[2 + side, 0, j], coef[2 + side, 1, j]),
-                    (ends[side, 0, j], ends[side, 1, j]),
-                ),
-            )
-            for p in range(2):
-                own_out[sweep, side, j, p] = base[p]
-
-            @pl.when(both(even[side], onward[side] >= 1))
+            if sweep == 0:
+                for p in range(2):
+                    own_out[sweep, side, j, p] = ends[1 - side, p, j]
+                    extra_out[side, j, p] = ends[side, p, j]
+            else:
+                base = own_base(side, j)
+                for p in range(2):
+                    own_out[sweep, side, j, p] = base[p]
+            sends = both(even[side], onward[side] >= 1)
+
+            @pl.when(sends)
             def _():
                 own_copy(sweep, side, j).start()
+
+            if sweep == 0:
+
+                @pl.when(both(sends, place[side] > 0))
+                def _():
+                    extra_copy(side, j).start()
 
     def pass_chain(sweep, side):
         for j in range(3):
+            base = own_base(side, j)
 
             @pl.when(odd[side])
             def _():
                 own_copy(sweep, side, j).wait_recv()
 
+            if sweep == 0:
+
+                @pl.when(both(odd[side], place[side] >= 2))
+                def _():
+                    extra_copy(side, j).wait_recv()
+
             @pl.when(place[side] >= 2)
             def _():
                 x_copy(sweep, side, 1, j).wait_recv()
@@ -407,6 +450,9 @@
             @pl.when(odd[side])
             def _():
                 own = (own_in[sweep, side, j, 0], own_in[sweep, side, j, 1])
+                if sweep == 0:
+                    extra = (extra_in[side, j, 0], extra_in[side, j, 1])
+                    own = add(own, mul((coef[12 + side, 0, j], coef[12 + side, 1, j]), extra))
                 x = add(own, mul((coef[8 + side, 0, j], coef[8 + side, 1, j]), given))
                 for p in range(2):
                     value_in[side, j, p] = x[p]
@@ -417,7 +463,6 @@
                     value_in[side, j, p] = given[p]
 
             x = (value_in[side, j, 0], value_in[side, j, 1])
-            base = (own_out[sweep, side, j, 0], own_out[sweep, side, j, 1])
             result = add(base, mul((coef[side, 0, j], coef[side, 1, j]), x))
             for p in range(2):
                 ch_out[sweep, side, j, p] = result[p]
@@ -448,10 +493,8 @@
         def _():
             run(LEFT)
 
-
     near_side(send_info)
     far_side(send_info)
-
 
     angle_matrix = rotation(angles, (rows, 128))
     for c in range(3):
@@ -514,12 +557,9 @@
         put(T, add(get(T, z), turned), z)
         return add(first, mul(get(PHI, z), turned)), add(last, mul(get(PSI, z), turned))
 
-
     loads[3].wait()
     for sweep in range(SWEEPS):
-
-        sums = lax.fori_loop(0, depth, inner, (none, none))
-
+        sums = loop(0, depth, inner, (none, none), 4)
         for piece in range(PIECES):
             for side in range(2):
 
@@ -527,22 +567,17 @@
                 def _():
                     halo_copy(sweep, side, piece).wait_recv()
 
-            sums = lax.fori_loop(
-                piece * zs, (piece + 1) * zs, functools.partial(outer, sweep), sums
+            sums = loop(
+                piece * zs, (piece + 1) * zs, functools.partial(outer, sweep), sums, 4
             )
         put(ends, sums[0], 0)
         put(ends, sums[1], 1)
 
-
+        near_side(functools.partial(own_sum, sweep))
+        far_side(functools.partial(own_sum, sweep))
         if sweep == 0:
             near_side(pass_lam)
-        near_side(functools.partial(own_sum, sweep))
-        if sweep > 0:
-            far_side(functools.partial(own_sum, sweep))
         near_side(functools.partial(pass_chain, sweep))
-        if sweep == 0:
-            far_side(pass_lam)
-            far_side(functools.partial(own_sum, sweep))
 
         def forward(z, m):
             m = mul(get(PH, z), add(get(T, z), m))
@@ -555,11 +590,10 @@
             put(T, w, z)
             return w
 
-
-        lax.fori_loop(0, depth, forward, none)
-        lax.fori_loop(0, depth, backward, none)
-
+        loop(0, depth, forward, none, 4)
+        loop(0, depth, backward, none, 4)
         if sweep == 0:
+            far_side(pass_lam)
             for side in range(2):
                 lam = get(coef, 10 + side)
                 away = tuple(
@@ -569,7 +603,6 @@
                 put(coef, det, 6 + side)
                 put(coef, mul(det, lam), 4 + side)
         far_side(functools.partial(pass_chain, sweep))
-
 
         for side in range(2):
             for j in range(3):
@@ -599,16 +632,14 @@
                 pack(sweep + 1, z, values)
             return carry
 
-
         for piece in range(PIECES):
-            lax.fori_loop(piece * zs, (piece + 1) * zs, join, 0)
+            loop(piece * zs, (piece + 1) * zs, join, 0, 4)
             if final:
                 span = pl.ds(piece * zs, zs)
                 pltpu.make_async_copy(OUT.at[span], out.at[span], out_sems.at[piece]).start()
             else:
                 send_halo(sweep + 1, piece)
 
-
     for side in range(2):
 
         @pl.when(has["xy", 1 - side])
@@ -630,6 +661,8 @@
         def _():
             for j in range(3, 9):
                 info_copy(side, j).wait_send()
+            for j in range(3):
+                extra_copy(side, j).wait_send()
 
         for steps in (2, 1):
 
@@ -674,13 +707,15 @@
             block,
             pltpu.VMEM((3, 3, rows, 128), f32),
             pltpu.VMEM((2,) + line, f32),
-            pltpu.VMEM((12,) + line, f32),
+            pltpu.VMEM((14,) + line, f32),
             pltpu.VMEM((2,) + line, f32),
             pltpu.VMEM((SWEEPS, 2, depth * 6, width), f32),
             pltpu.VMEM((SWEEPS, 2, depth * 6, width), f32),
             pltpu.VMEM((2, 3) + pair, f32),
             pltpu.VMEM((2, 9) + pair, f32),
             pltpu.VMEM((2, 9) + pair, f32),
+            pltpu.VMEM((2, 3) + pair, f32),
+            pltpu.VMEM((2, 3) + pair, f32),
             pltpu.VMEM((2, 3) + pair, f32),
             pltpu.VMEM((2, 3) + pair, f32),
             pltpu.VMEM((SWEEPS, 2, 3) + pair, f32),
@@ -695,6 +730,8 @@
             dma((2, 9)),
             dma((2, 2, 3)),
             dma((2, 3)),
+            dma((2, 3)),
+            dma((2, 3)),
             dma((SWEEPS, 2, 3)),
             dma((SWEEPS, 2, 3)),
             dma((SWEEPS, 2, 2, 3)),

time: 32.7 us -> 30 us (0.917)
  the two profiles are of different devices: /device:TPU:0 before, /device:TPU:4 now
where the time goes in v2:
time: 30 us; the launch traced here: 29.9 us
  Pallas kernels  27.8 us (93%)
  local copies, waits for them, and re-layouts  2.06 us (7%)
    pallas_call x1, Pallas kernels, local(): pl.pallas_call(functools.partial(relax, ngz, nxy), out_shape=jax.ShapeDty...  27.8 us
    unnamed x1, local copies, waits for them, and re-layouts  2.06 us

profile of v2, /device:TPU:4, one launch (start us, length us, event | category | flops | bytes accessed | tf_op | source)
XLA Modules:
  0.0 29.9 jit_solution(9500780329628575653)
XLA Ops:
  0.0 27.8 %shard_map.73 = f32[16,2,3,8,256]{4,3,2,1,0:T(8,128)} custom-call(f32[16,2,3,8,256]{4,3,2,1,0:T(8,128)} %field.1, f32[16,2,3,8,256]{4,3,2,1,0:T(8,128)} %source.1, s32[16,8,256]{2,1,0:T(8,128)} %classes.1, s32[16,8,256]{2,1,0:T(8,128)} %boundary.1, f32[16]{0:T(128)} %conductance.1, f32[3]{0:T(128)} %angles.1, f32[3]{0:T(128)} %strengths.1), custom_call_target="tpu_custom_call" | custom-call | tf_op jit(solution)/shard_map/pallas_call | solution.py:691
  27.8 2.1 %copy.9 = f32[16,2,3,8,256]{4,3,2,1,0:T(8,128)} copy(f32[16,2,3,8,256]{4,3,2,1,0:T(8,128)} %shard_map.73) | data formatting | bytes 1572864

commit v3 on v2

--- a/solution.py
+++ b/solution.py
@@ -9,6 +9,7 @@
 
 SWEEPS = 2
 PIECES = 2
+VMEM_LIMIT = 62 * 2**20
 
 coupling = 0.1
 penalty = 4.0
@@ -69,7 +70,7 @@
     conductance,
     angles,
     strengths,
-    out,
+    OUT,
     U,
     S,
     C,
@@ -80,7 +81,6 @@
     PHI,
     PSI,
     T,
-    OUT,
     QM,
     ends,
     coef,
@@ -99,7 +99,6 @@
     ch_in,
     ch_out,
     in_sems,
-    out_sems,
     halo_send,
     halo_recv,
     info_send,
@@ -634,10 +633,7 @@
 
         for piece in range(PIECES):
             loop(piece * zs, (piece + 1) * zs, join, 0, 4)
-            if final:
-                span = pl.ds(piece * zs, zs)
-                pltpu.make_async_copy(OUT.at[span], out.at[span], out_sems.at[piece]).start()
-            else:
+            if not final:
                 send_halo(sweep + 1, piece)
 
     for side in range(2):
@@ -672,10 +668,6 @@
                     lam_copy(side, steps, j).wait_send()
                     for sweep in range(SWEEPS):
                         x_copy(sweep, side, steps, j).wait_send()
-
-    for piece in range(PIECES):
-        span = pl.ds(piece * zs, zs)
-        pltpu.make_async_copy(OUT.at[span], out.at[span], out_sems.at[piece]).wait()
 
 
 def local(ngz, nxy, field, source, classes, boundary, conductance, angles, strengths):
@@ -690,9 +682,9 @@
     smem = pl.BlockSpec(memory_space=pltpu.SMEM)
     return pl.pallas_call(
         functools.partial(relax, ngz, nxy),
-        out_shape=jax.ShapeDtypeStruct(field.shape, f32),
+        out_shape=pltpu.VMEM(field.shape, f32),
         in_specs=[hbm] * 4 + [smem] * 3,
-        out_specs=hbm,
+        out_specs=pl.BlockSpec(memory_space=pltpu.VMEM),
         scratch_shapes=[
             block,
             block,
@@ -700,7 +692,6 @@
             pltpu.VMEM(flat, jnp.int32),
             pltpu.VMEM(flat, f32),
             pltpu.VMEM(flat, f32),
-            block,
             block,
             block,
             block,
@@ -723,7 +714,6 @@
             pltpu.VMEM((SWEEPS, 2, 3) + pair, f32),
             pltpu.VMEM((SWEEPS, 2, 3) + pair, f32),
             dma((4,)),
-            dma((PIECES,)),
             dma((SWEEPS, 2, PIECES)),
             dma((SWEEPS, 2, PIECES)),
             dma((2, 9)),
@@ -737,7 +727,7 @@
             dma((SWEEPS, 2, 2, 3)),
             dma((SWEEPS, 2, 3)),
         ],
-        compiler_params=pltpu.CompilerParams(collective_id=0, has_side_effects=True),
+        compiler_params=pltpu.CompilerParams(collective_id=0, has_side_effects=True, vmem_limit_bytes=VMEM_LIMIT),
     )(field, source, classes, boundary, conductance, angles, strengths)
 
 

time: 30 us -> 28.2 us (0.940)
  local copies, waits for them, and re-layouts: 2.06 us -> 0.88 us
  Pallas kernels: 27.8 us -> 27.1 us
    unnamed x1, local copies, waits for them, and re-layouts: 2.06 us -> 0.88 us
    pallas_call x1, Pallas kernels: 27.8 us -> 27.1 us  [local(): pl.pallas_call(functools.partial(relax, ngz, nxy), out_shape=pltpu.VMEM(f...]
where the time goes in v3:
time: 28.2 us; the launch traced here: 28 us
  Pallas kernels  27.1 us (96%)
  local copies, waits for them, and re-layouts  0.88 us (3%)
    pallas_call x1, Pallas kernels, local(): pl.pallas_call(functools.partial(relax, ngz, nxy), out_shape=pltpu.VMEM(f...  27.1 us
    unnamed x1, local copies, waits for them, and re-layouts  0.88 us

profile of v3, /device:TPU:4, one launch (start us, length us, event | category | flops | bytes accessed | tf_op | source)
XLA Modules:
  0.0 28.0 jit_solution(12290517607483185596)
XLA Ops:
  0.0 27.1 %shard_map.73 = f32[16,2,3,8,256]{4,3,2,1,0:T(8,128)S(1)} custom-call(f32[16,2,3,8,256]{4,3,2,1,0:T(8,128)} %field.1, f32[16,2,3,8,256]{4,3,2,1,0:T(8,128)} %source.1, s32[16,8,256]{2,1,0:T(8,128)} %classes.1, s32[16,8,256]{2,1,0:T(8,128)} %boundary.1, f32[16]{0:T(128)} %conductance.1, f32[3]{0:T(128)} %angles.1, f32[3]{0:T(128)} %strengths.1), custom_call_target="tpu_custom_call" | custom-call | tf_op jit(solution)/shard_map/pallas_call | solution.py:683
  27.1 0.9 %copy.9 = f32[16,2,3,8,256]{4,3,2,1,0:T(8,128)} copy(f32[16,2,3,8,256]{4,3,2,1,0:T(8,128)S(1)} %shard_map.73) | data formatting | bytes 1572864

commit v4 on v3

--- a/solution.py
+++ b/solution.py
@@ -82,6 +82,10 @@
     PSI,
     T,
     QM,
+    EPHI,
+    EPSI,
+    EH,
+    ET,
     ends,
     coef,
     near,
@@ -129,9 +133,12 @@
         has["gz", steps] = iz < ngz - steps
         where_is["gz", -steps] = iz - steps
         where_is["gz", steps] = iz + steps
+    zs = depth // PIECES
+    spans = [pl.ds(piece * zs, zs) for piece in range(PIECES)]
+    moves = [(field.at[span], U.at[span]) for span in spans]
+    moves += [(classes, C), (boundary, B), (source, S)]
     loads = [
-        pltpu.make_async_copy(src, dst, in_sems.at[i])
-        for i, (src, dst) in enumerate(((field, U), (classes, C), (boundary, B), (source, S)))
+        pltpu.make_async_copy(src, dst, in_sems.at[i]) for i, (src, dst) in enumerate(moves)
     ]
     for load in loads:
         load.start()
@@ -159,14 +166,11 @@
             device_id_type=pl.DeviceIdType.MESH,
         )
 
-    zs = depth // PIECES
-    lines = zs * 6
-
     def halo_copy(sweep, side, piece):
-        span = pl.ds(piece * lines, lines)
+        span = pl.ds(piece * zs, zs)
         return remote(
-            halo_out.at[sweep, side, span],
-            halo_in.at[sweep, side, span],
+            halo_out.at[sweep, side, :, :, span],
+            halo_in.at[sweep, side, :, :, span],
             halo_send.at[sweep, side, piece],
             halo_recv.at[sweep, side, piece],
             ("xy", 1 - side),
@@ -179,10 +183,11 @@
             def _():
                 halo_copy(sweep, side, piece).start()
 
-    def pack(sweep, z, values):
+    def pack(first, last, z, values):
         for i in range(6):
-            halo_out[sweep, 0, pl.ds(z * 6 + i, 1), :] = values[i][rows - 1 :, :]
-            halo_out[sweep, 1, pl.ds(z * 6 + i, 1), :] = values[i][:1, :]
+            at = (i // 3, i % 3, pl.ds(z, 1), slice(None))
+            first[at] = values[i][:1, :]
+            last[at] = values[i][rows - 1 :, :]
 
     for side in range(2):
 
@@ -201,20 +206,22 @@
                 for j in range(3):
                     ch_in[sweep, side, j] = jnp.zeros(ch_in.shape[3:], jnp.float32)
 
-    loads[0].wait()
+    count = sum(there.astype(jnp.int32) for there in has.values())
 
     def pack_first(z, carry):
-        pack(0, z, [U[z, i // 3, i % 3] for i in range(6)])
+        values = [U[z, i // 3, i % 3] for i in range(6)]
+        pack(halo_out.at[0, 1], halo_out.at[0, 0], z, values)
         return carry
 
-    loop(0, depth, pack_first, 0, 4)
-    count = sum(there.astype(jnp.int32) for there in has.values())
-    pl.semaphore_wait(barrier, count)
     for piece in range(PIECES):
+        loads[piece].wait()
+        loop(piece * zs, (piece + 1) * zs, pack_first, 0, 4)
+        if piece == 0:
+            pl.semaphore_wait(barrier, count)
         send_halo(0, piece)
 
-    loads[1].wait()
-    loads[2].wait()
+    loads[PIECES].wait()
+    loads[PIECES + 1].wait()
 
     def diagonal(z, carry):
         ids = C[z]
@@ -466,11 +473,14 @@
             for p in range(2):
                 ch_out[sweep, side, j, p] = result[p]
 
-            for steps in (2, 1):
-
-                @pl.when(both(odd[side], onward[side] >= steps))
-                def _():
-                    x_copy(sweep, side, steps, j).start()
+            @pl.when(both(odd[side], onward[side] >= 2))
+            def _():
+                x_copy(sweep, side, 2, j).start()
+
+        @pl.when(both(odd[side], onward[side] >= 1))
+        def _():
+            for j in range(3):
+                x_copy(sweep, side, 1, j).start()
 
     left_first = iz * 2 < ngz - 1
 
@@ -505,6 +515,13 @@
             [jnp.concatenate([QM[c, j]] * (width // 128), axis=1) for j in range(3)]
             for c in range(3)
         ]
+
+    def pack_columns(z, carry):
+        for src, dst in ((PHI, EPHI), (PSI, EPSI)):
+            pack(dst.at[0], dst.at[1], z, [src[z, i // 3, i % 3] for i in range(6)])
+        return carry
+
+    loop(0, depth, pack_columns, 0, 4)
 
     row = lax.broadcasted_iota(jnp.int32, plane, 0)
     lane = lax.broadcasted_iota(jnp.int32, plane, 1)
@@ -539,26 +556,25 @@
         put(T, turned, z)
         return add(first, mul(get(PHI, z), turned)), add(last, mul(get(PSI, z), turned))
 
-    def outer(sweep, z, carry):
+    tiles = [pl.ds(z, rows) for z in range(0, depth, rows)]
+
+    def outer(sweep, side, tile, carry):
         first, last = carry
         q = matrix()
-        driven = []
+        turned = turn(
+            q,
+            [[coupling * halo_in[sweep, side, p, c, tile] for c in range(3)] for p in range(2)],
+        )
         for p in range(2):
-            of = []
-            for c in range(3):
-                at = pl.ds(z * 6 + p * 3 + c, 1)
-                above = jnp.broadcast_to(halo_in[sweep, 0, at, :], plane)
-                below = jnp.broadcast_to(halo_in[sweep, 1, at, :], plane)
-                edge = jnp.where(row == 0, above, zero) + jnp.where(row == rows - 1, below, zero)
-                of.append(coupling * edge)
-            driven.append(of)
-        turned = turn(q, driven)
-        put(T, add(get(T, z), turned), z)
-        return add(first, mul(get(PHI, z), turned)), add(last, mul(get(PSI, z), turned))
-
-    loads[3].wait()
+            EH[side, p, :, tile] = turned[p]
+        phi = [EPHI[side, p, :, tile] for p in range(2)]
+        psi = [EPSI[side, p, :, tile] for p in range(2)]
+        return add(first, mul(phi, turned)), add(last, mul(psi, turned))
+
+    loads[PIECES + 2].wait()
     for sweep in range(SWEEPS):
         sums = loop(0, depth, inner, (none, none), 4)
+        halves = [(none, none), (none, none)]
         for piece in range(PIECES):
             for side in range(2):
 
@@ -566,8 +582,19 @@
                 def _():
                     halo_copy(sweep, side, piece).wait_recv()
 
-            sums = loop(
-                piece * zs, (piece + 1) * zs, functools.partial(outer, sweep), sums, 4
+                for tile in tiles[piece * len(tiles) // PIECES : (piece + 1) * len(tiles) // PIECES]:
+                    halves[side] = outer(sweep, side, tile, halves[side])
+        for side in range(2):
+            here = row == (0 if side == 0 else rows - 1)
+            sums = tuple(
+                add(
+                    sums[end],
+                    tuple(
+                        jnp.where(here[None], jnp.sum(part, axis=1, keepdims=True), 0.0)
+                        for part in halves[side][end]
+                    ),
+                )
+                for end in range(2)
             )
         put(ends, sums[0], 0)
         put(ends, sums[1], 1)
@@ -579,7 +606,17 @@
         near_side(functools.partial(pass_chain, sweep))
 
         def forward(z, m):
-            m = mul(get(PH, z), add(get(T, z), m))
+            given = []
+            for p in range(2):
+                edges = []
+                for j in range(3):
+                    above = jnp.broadcast_to(EH[0, p, j, pl.ds(z, 1), :], plane)
+                    below = jnp.broadcast_to(EH[1, p, j, pl.ds(z, 1), :], plane)
+                    edges.append(
+                        jnp.where(row == 0, above, zero) + jnp.where(row == rows - 1, below, zero)
+                    )
+                given.append(T[z, p] + jnp.stack(edges))
+            m = mul(get(PH, z), add(given, m))
             put(T, m, z)
             return m
 
@@ -587,6 +624,8 @@
             z = depth - 1 - k
             w = add(get(T, z), mul(get(PH, z), w))
             put(T, w, z)
+            if sweep < SWEEPS - 1:
+                pack(ET.at[0], ET.at[1], z, [w[i // 3][i % 3] for i in range(6)])
             return w
 
         loop(0, depth, forward, none, 4)
@@ -616,6 +655,30 @@
 
         final = sweep == SWEEPS - 1
 
+        def join_edge(side, tile):
+            q = matrix()
+            r = 0 if side == 0 else rows - 1
+            w = [ET[side, p, :, tile] for p in range(2)]
+            for end, column in ((0, EPHI), (1, EPSI)):
+                entry = [
+                    jnp.broadcast_to(near[end, p, :, r : r + 1, :], (3,) + plane)
+                    for p in range(2)
+                ]
+                w = add(w, mul([column[side, p, :, tile] for p in range(2)], entry))
+            for p in range(2):
+                for c in range(3):
+                    halo_out[sweep + 1, 1 - side, p, c, tile] = (
+                        q[c][0] * w[p][0] + q[c][1] * w[p][1] + q[c][2] * w[p][2]
+                    )
+
+        if not final:
+            for piece in range(PIECES):
+                for tile in tiles[piece * len(tiles) // PIECES : (piece + 1) * len(tiles) // PIECES]:
+                    for side in range(2):
+                        join_edge(side, tile)
+                send_halo(sweep + 1, piece)
+
+
         def join(z, carry):
             q = matrix()
             before, after = get(near, 0), get(near, 1)
@@ -627,14 +690,9 @@
             target = OUT if final else U
             for i in range(6):
                 target[z, i // 3, i % 3] = values[i]
-            if not final:
-                pack(sweep + 1, z, values)
             return carry
 
-        for piece in range(PIECES):
-            loop(piece * zs, (piece + 1) * zs, join, 0, 4)
-            if not final:
-                send_halo(sweep + 1, piece)
+        loop(0, depth, join, 0, 4)
 
     for side in range(2):
 
@@ -677,6 +735,7 @@
     flat = (depth, rows, width)
     line = (2, 3, rows, width)
     pair = (2, rows, width)
+    edge = (2, 2, 3, depth, width)
     dma = pltpu.SemaphoreType.DMA
     hbm = pl.BlockSpec(memory_space=pl.ANY)
     smem = pl.BlockSpec(memory_space=pltpu.SMEM)
@@ -697,11 +756,15 @@
             block,
             block,
             pltpu.VMEM((3, 3, rows, 128), f32),
+            pltpu.VMEM(edge, f32),
+            pltpu.VMEM(edge, f32),
+            pltpu.VMEM(edge, f32),
+            pltpu.VMEM(edge, f32),
             pltpu.VMEM((2,) + line, f32),
             pltpu.VMEM((14,) + line, f32),
             pltpu.VMEM((2,) + line, f32),
-            pltpu.VMEM((SWEEPS, 2, depth * 6, width), f32),
-            pltpu.VMEM((SWEEPS, 2, depth * 6, width), f32),
+            pltpu.VMEM((SWEEPS,) + edge, f32),
+            pltpu.VMEM((SWEEPS,) + edge, f32),
             pltpu.VMEM((2, 3) + pair, f32),
             pltpu.VMEM((2, 9) + pair, f32),
             pltpu.VMEM((2, 9) + pair, f32),
@@ -713,7 +776,7 @@
             pltpu.VMEM((SWEEPS, 2, 3) + pair, f32),
             pltpu.VMEM((SWEEPS, 2, 3) + pair, f32),
             pltpu.VMEM((SWEEPS, 2, 3) + pair, f32),
-            dma((4,)),
+            dma((PIECES + 3,)),
             dma((SWEEPS, 2, PIECES)),
             dma((SWEEPS, 2, PIECES)),
             dma((2, 9)),

time: 28.2 us -> 26.8 us (0.950)
  Pallas kernels: 27.1 us -> 25.7 us
    pallas_call x1, Pallas kernels: 27.1 us -> 25.7 us  [local(): pl.pallas_call(functools.partial(relax, ngz, nxy), out_shape=pltpu.VMEM(f...]
where the time goes in v4:
time: 26.8 us; the launch traced here: 26.6 us
  Pallas kernels  25.7 us (96%)
  local copies, waits for them, and re-layouts  0.88 us (3%)
    pallas_call x1, Pallas kernels, local(): pl.pallas_call(functools.partial(relax, ngz, nxy), out_shape=pltpu.VMEM(f...  25.7 us
    unnamed x1, local copies, waits for them, and re-layouts  0.88 us

profile of v4, /device:TPU:4, one launch (start us, length us, event | category | flops | bytes accessed | tf_op | source)
XLA Modules:
  0.0 26.6 jit_solution(7845372027874973792)
XLA Ops:
  0.0 25.7 %shard_map.73 = f32[16,2,3,8,256]{4,3,2,1,0:T(8,128)S(1)} custom-call(f32[16,2,3,8,256]{4,3,2,1,0:T(8,128)} %field.1, f32[16,2,3,8,256]{4,3,2,1,0:T(8,128)} %source.1, s32[16,8,256]{2,1,0:T(8,128)} %classes.1, s32[16,8,256]{2,1,0:T(8,128)} %boundary.1, f32[16]{0:T(128)} %conductance.1, f32[3]{0:T(128)} %angles.1, f32[3]{0:T(128)} %strengths.1), custom_call_target="tpu_custom_call" | custom-call | tf_op jit(solution)/shard_map/pallas_call | solution.py:742
  25.7 0.9 %copy.9 = f32[16,2,3,8,256]{4,3,2,1,0:T(8,128)} copy(f32[16,2,3,8,256]{4,3,2,1,0:T(8,128)S(1)} %shard_map.73) | data formatting | bytes 1572864

commit v5 on v4

--- a/solution.py
+++ b/solution.py
@@ -140,7 +140,7 @@
     loads = [
         pltpu.make_async_copy(src, dst, in_sems.at[i]) for i, (src, dst) in enumerate(moves)
     ]
-    for load in loads:
+    for load in loads[:-1]:
         load.start()
 
     barrier = pltpu.get_barrier_semaphore()
@@ -215,6 +215,8 @@
 
     for piece in range(PIECES):
         loads[piece].wait()
+        if piece == PIECES - 1:
+            loads[-1].start()
         loop(piece * zs, (piece + 1) * zs, pack_first, 0, 4)
         if piece == 0:
             pl.semaphore_wait(barrier, count)
@@ -386,11 +388,14 @@
                 coef[2 + side, p, j] = over[p]
                 lam_out[side, j, p] = value[p]
 
-            for steps in (2, 1):
-
-                @pl.when(both(odd[side], onward[side] >= steps))
-                def _():
-                    lam_copy(side, steps, j).start()
+            @pl.when(both(odd[side], onward[side] >= 2))
+            def _():
+                lam_copy(side, 2, j).start()
+
+        @pl.when(both(odd[side], onward[side] >= 1))
+        def _():
+            for j in range(3):
+                lam_copy(side, 1, j).start()
 
     def extra_copy(side, j):
         return chain_copy(

time: 26.8 us -> 26.8 us (level)
  no operation moved by 1% of the time
where the time goes in v5:
time: 26.8 us; the launch traced here: 26.6 us
  Pallas kernels  25.7 us (96%)
  local copies, waits for them, and re-layouts  0.88 us (3%)
    pallas_call x1, Pallas kernels, local(): pl.pallas_call(functools.partial(relax, ngz, nxy), out_shape=pltpu.VMEM(f...  25.7 us
    unnamed x1, local copies, waits for them, and re-layouts  0.88 us

profile of v5, /device:TPU:4, one launch (start us, length us, event | category | flops | bytes accessed | tf_op | source)
XLA Modules:
  0.0 26.6 jit_solution(18196221284627194100)
XLA Ops:
  0.0 25.7 %shard_map.73 = f32[16,2,3,8,256]{4,3,2,1,0:T(8,128)S(1)} custom-call(f32[16,2,3,8,256]{4,3,2,1,0:T(8,128)} %field.1, f32[16,2,3,8,256]{4,3,2,1,0:T(8,128)} %source.1, s32[16,8,256]{2,1,0:T(8,128)} %classes.1, s32[16,8,256]{2,1,0:T(8,128)} %boundary.1, f32[16]{0:T(128)} %conductance.1, f32[3]{0:T(128)} %angles.1, f32[3]{0:T(128)} %strengths.1), custom_call_target="tpu_custom_call" | custom-call | tf_op jit(solution)/shard_map/pallas_call | solution.py:747
  25.7 0.9 %copy.9 = f32[16,2,3,8,256]{4,3,2,1,0:T(8,128)} copy(f32[16,2,3,8,256]{4,3,2,1,0:T(8,128)S(1)} %shard_map.73) | data formatting | bytes 1572864

commit v6 on v5

--- a/solution.py
+++ b/solution.py
@@ -579,6 +579,8 @@
     loads[PIECES + 2].wait()
     for sweep in range(SWEEPS):
         sums = loop(0, depth, inner, (none, none), 4)
+        if sweep == 0:
+            near_side(pass_lam)
         halves = [(none, none), (none, none)]
         for piece in range(PIECES):
             for side in range(2):
@@ -606,8 +608,6 @@
 
         near_side(functools.partial(own_sum, sweep))
         far_side(functools.partial(own_sum, sweep))
-        if sweep == 0:
-            near_side(pass_lam)
         near_side(functools.partial(pass_chain, sweep))
 
         def forward(z, m):

time: 26.8 us -> 26.5 us (0.989)
  Pallas kernels: 25.7 us -> 25.4 us
    pallas_call x1, Pallas kernels: 25.7 us -> 25.4 us  [local(): pl.pallas_call(functools.partial(relax, ngz, nxy), out_shape=pltpu.VMEM(f...]
where the time goes in v6:
time: 26.5 us; the launch traced here: 26.3 us
  Pallas kernels  25.4 us (96%)
  local copies, waits for them, and re-layouts  0.88 us (3%)
    pallas_call x1, Pallas kernels, local(): pl.pallas_call(functools.partial(relax, ngz, nxy), out_shape=pltpu.VMEM(f...  25.4 us
    unnamed x1, local copies, waits for them, and re-layouts  0.88 us

profile of v6, /device:TPU:4, one launch (start us, length us, event | category | flops | bytes accessed | tf_op | source)
XLA Modules:
  0.0 26.3 jit_solution(7472285157062407205)
XLA Ops:
  0.0 25.4 %shard_map.73 = f32[16,2,3,8,256]{4,3,2,1,0:T(8,128)S(1)} custom-call(f32[16,2,3,8,256]{4,3,2,1,0:T(8,128)} %field.1, f32[16,2,3,8,256]{4,3,2,1,0:T(8,128)} %source.1, s32[16,8,256]{2,1,0:T(8,128)} %classes.1, s32[16,8,256]{2,1,0:T(8,128)} %boundary.1, f32[16]{0:T(128)} %conductance.1, f32[3]{0:T(128)} %angles.1, f32[3]{0:T(128)} %strengths.1), custom_call_target="tpu_custom_call" | custom-call | tf_op jit(solution)/shard_map/pallas_call | solution.py:747
  25.4 0.9 %copy.9 = f32[16,2,3,8,256]{4,3,2,1,0:T(8,128)} copy(f32[16,2,3,8,256]{4,3,2,1,0:T(8,128)S(1)} %shard_map.73) | data formatting | bytes 1572864
